TPU v7x, 32 devices: a whole 2x2x4 slice. The times are simulated.
32 devices in a mesh: dp: 4 (over x, core), fsdp: 8 (over z, y).
Axes of the slice: x: 2, y: 2, z: 4, core: 2. Of those that a mesh axis runs over, the one named last changes fastest.
Arguments:
- text_rows: bfloat16 [64, 512, 768], P(('dp', 'fsdp')), may hold values from -6 to 6
- visual_matrix: bfloat16 [768, 768], P('fsdp'), may hold values from -0.21875 to 0.21875
- batch_gain: bfloat16 [768], P('fsdp'), may hold values from 0.5 to 1.5
- batch_shift: bfloat16 [768], P('fsdp'), may hold values from -2.5 to 2.5
- attend_weight: bfloat16 [768, 2304], P('fsdp'), may hold values from -0.21875 to 0.21875
- merge_weight: bfloat16 [768, 768], P('fsdp'), may hold values from -1.75 to 1.75
- first_gain: bfloat16 [768], P('fsdp'), may hold values from 0.5 to 1.5
- first_shift: bfloat16 [768], P('fsdp'), may hold values from -2.5 to 2.5
- up_matrix: bfloat16 [768, 3072], P('fsdp'), may hold values from -0.21875 to 0.21875
- down_matrix: bfloat16 [3072, 768], P('fsdp'), may hold values from -0.109375 to 0.109375
- second_gain: bfloat16 [768], P('fsdp'), may hold values from 0.5 to 1.5
- second_shift: bfloat16 [768], P('fsdp'), may hold values from -2.5 to 2.5
- segment_counts: int32 [64], P(('dp', 'fsdp')), may hold values from 5 to 128, as said below
- segment_ids: int32 [64, 512], P(('dp', 'fsdp')), may hold values from -1 to 127, as said below
- padding_mask: int32 [64, 512], P(('dp', 'fsdp')), may hold values from 0 to 1, as said below
- cotangent: bfloat16 [64, 512, 768], P(('dp', 'fsdp')), may hold values from -6 to 6
Outputs:
- layer_output: float32 [64, 512, 768], P(('dp', 'fsdp'))
- text_gradient: float32 [64, 512, 768], P(('dp', 'fsdp'))
- visual_gradient: float32 [768, 768], P('fsdp')
- batch_gain_gradient: float32 [768], P('fsdp')
- batch_shift_gradient: float32 [768], P('fsdp')
- attend_gradient: float32 [768, 2304], P('fsdp')
- merge_gradient: float32 [768, 768], P('fsdp')
- first_gain_gradient: float32 [768], P('fsdp')
- first_shift_gradient: float32 [768], P('fsdp')
- up_gradient: float32 [768, 3072], P('fsdp')
- down_gradient: float32 [3072, 768], P('fsdp')
- second_gain_gradient: float32 [768], P('fsdp')
- second_shift_gradient: float32 [768], P('fsdp')
Inputs may be any that keep to these rules, and one draw needn't show every extreme that they name: On every device of dp+fsdp one of its documents has exactly 128 segments; segment_counts[d] is one more than the largest segment_ids in document d. `segment_ids`: A document's real rows come first and form segment_counts consecutive runs of one or more rows, numbered 0, 1, ... in order; padding rows hold -1. `padding_mask`: 1 exactly on the rows whose segment id is not -1, which are the first 256 or more rows of a document.
All inputs are finite; a program needn't handle non-finite values.
Results may differ from a plain program's by a relative error of at most 0.023.
The roundings to bfloat16 on the way count: a program that leaves them out, or rounds other values in their place, can miss the bound.
Values may be sent and summed in bfloat16 or wider, within the bound.
No kernel may reach another device: no remote copies, remote signals or barrier semaphores. Data moves between devices by JAX's collectives and lax.ppermute only.
A program may use at most 192 MiB of HBM per device.

v0:
```python
import jax
import jax.numpy as jnp
from jax import lax
from jax.sharding import PartitionSpec as P

HEADS = 12
SEGMAX = 128
eps_norm = 1e-05
eps_batch = 1e-05
masked_score = -1e30
highest_precision = lax.Precision.HIGHEST


def layer_norm(values, gain, shift):
    center = values - jnp.mean(values, axis=-1, keepdims=True)
    variance = jnp.mean(center * center, axis=-1, keepdims=True)
    return center * lax.rsqrt(variance + eps_norm) * gain + shift


def exact_gelu(values):
    return jax.nn.gelu(values, approximate=False)


def split_heads(packed):
    length = packed.shape[0]
    features = packed.shape[1] // 3
    head_size = features // HEADS
    queries = packed[:, :features].reshape(length, HEADS, head_size)
    keys_part = packed[:, features : 2 * features].reshape(length, HEADS, head_size)
    values_part = packed[:, 2 * features :].reshape(length, HEADS, head_size)
    return (queries, keys_part, values_part, head_size ** (-0.5))


def masked_scores(queries, keys_part, key_mask, scaling):
    scores = (
        jnp.einsum("qhe,khe->hqk", queries, keys_part, preferred_element_type=jnp.float32) * scaling
    )
    return jnp.where(key_mask[None, None, :] > 0, scores, masked_score)


def attend_doc(operands):
    packed, key_mask = operands
    queries, keys_part, values_part, scaling = split_heads(packed)
    scores = masked_scores(queries, keys_part, key_mask, scaling)
    top_score = jnp.max(scores, axis=-1, keepdims=True)
    unnormed = jnp.exp(scores - top_score)
    totals = jnp.sum(unnormed, axis=-1, keepdims=True)
    attention = unnormed / totals
    mixed = jnp.einsum(
        "hqk,khe->qhe",
        attention.astype(jnp.bfloat16),
        values_part,
        preferred_element_type=jnp.float32,
    )
    log_total = (top_score + jnp.log(totals))[..., 0]
    return (mixed.reshape(packed.shape[0], packed.shape[1] // 3).astype(jnp.bfloat16), log_total)


def attend_back(operands):
    packed, key_mask, log_total, delta_attended = operands
    queries, keys_part, values_part, scaling = split_heads(packed)
    length = packed.shape[0]
    features = packed.shape[1] // 3
    scores = masked_scores(queries, keys_part, key_mask, scaling)
    attention = jnp.exp(scores - log_total[..., None])
    delta_heads = delta_attended.reshape(length, HEADS, features // HEADS)
    delta_attention = jnp.einsum(
        "qhe,khe->hqk", delta_heads, values_part, preferred_element_type=jnp.float32
    )
    delta_scores = attention * (
        delta_attention - jnp.sum(attention * delta_attention, axis=-1, keepdims=True)
    )
    delta_low = delta_scores.astype(jnp.bfloat16)
    delta_queries = (
        jnp.einsum("hqk,khe->qhe", delta_low, keys_part, preferred_element_type=jnp.float32)
        * scaling
    )
    delta_keys = (
        jnp.einsum("hqk,qhe->khe", delta_low, queries, preferred_element_type=jnp.float32) * scaling
    )
    delta_values = jnp.einsum(
        "hqk,qhe->khe",
        attention.astype(jnp.bfloat16),
        delta_heads,
        preferred_element_type=jnp.float32,
    )
    merged = jnp.concatenate(
        [
            delta_queries.reshape(length, features),
            delta_keys.reshape(length, features),
            delta_values.reshape(length, features),
        ],
        axis=1,
    )
    return merged.astype(jnp.bfloat16)


def shards(
    text_rows,
    visual_matrix,
    batch_gain,
    batch_shift,
    attend_weight,
    merge_weight,
    first_gain,
    first_shift,
    up_matrix,
    down_matrix,
    second_gain,
    second_shift,
    segment_counts,
    segment_ids,
    padding_mask,
    cotangent,
):
    gathered = (
        lax.all_gather(visual_matrix, "fsdp", axis=0, tiled=True),
        lax.all_gather(batch_gain, "fsdp", axis=0, tiled=True),
        lax.all_gather(batch_shift, "fsdp", axis=0, tiled=True),
        lax.all_gather(attend_weight, "fsdp", axis=0, tiled=True),
        lax.all_gather(merge_weight, "fsdp", axis=0, tiled=True),
        lax.all_gather(first_gain, "fsdp", axis=0, tiled=True),
        lax.all_gather(first_shift, "fsdp", axis=0, tiled=True),
        lax.all_gather(up_matrix, "fsdp", axis=0, tiled=True),
        lax.all_gather(down_matrix, "fsdp", axis=0, tiled=True),
        lax.all_gather(second_gain, "fsdp", axis=0, tiled=True),
        lax.all_gather(second_shift, "fsdp", axis=0, tiled=True),
    )
    (
        gathered_visual_weight,
        full_batch_gain,
        full_batch_shift,
        full_attend,
        full_merge,
        full_first_gain,
        full_first_shift,
        gathered_up_weight,
        gathered_down_weight,
        full_second_gain,
        full_second_shift,
    ) = gathered
    features = text_rows.shape[2]
    slot_index = jnp.arange(SEGMAX)
    matches = segment_ids[:, :, None] == slot_index[None, None, :]
    onehot = matches.astype(jnp.bfloat16)
    onehot_wide = matches.astype(jnp.float32)
    divisor = jnp.maximum(jnp.sum(onehot_wide, axis=1), 1.0)[..., None]
    pooled_segments = (
        jnp.einsum("drs,drc->dsc", onehot, text_rows, preferred_element_type=jnp.float32) / divisor
    ).astype(jnp.bfloat16)
    visual_rows = jnp.einsum(
        "bil,ly->biy", pooled_segments, gathered_visual_weight, preferred_element_type=jnp.float32
    )
    valid_slot = (slot_index[None, :] < segment_counts[:, None]).astype(jnp.float32)[..., None]
    local_count = jnp.sum(segment_counts).astype(jnp.float32)
    masked_visual = valid_slot * visual_rows
    segment_total, visual_sum = lax.psum(
        (local_count, jnp.sum(masked_visual, axis=(0, 1))), ("dp", "fsdp")
    )
    batch_center = visual_sum / segment_total
    center = visual_rows - batch_center
    variance = (
        lax.psum(jnp.sum(valid_slot * center * center, axis=(0, 1)), ("dp", "fsdp")) / segment_total
    )
    inverse_spread = lax.rsqrt(variance + eps_batch)
    normed = center * inverse_spread
    embedded = (
        normed * full_batch_gain.astype(jnp.float32) + full_batch_shift.astype(jnp.float32)
    ).astype(jnp.bfloat16)
    joined = text_rows.astype(jnp.float32) + jnp.einsum(
        "drs,dsc->drc", onehot, embedded, preferred_element_type=jnp.float32
    )
    joined_low = joined.astype(jnp.bfloat16)
    packed = jnp.einsum(
        "drc,ce->dre", joined_low, full_attend, preferred_element_type=jnp.float32
    ).astype(jnp.bfloat16)
    attended, log_total = lax.map(attend_doc, (packed, padding_mask))
    projected = jnp.einsum("drc,ce->dre", attended, full_merge, preferred_element_type=jnp.float32)
    pre_one = joined + projected
    hidden_state = layer_norm(
        pre_one, full_first_gain.astype(jnp.float32), full_first_shift.astype(jnp.float32)
    )
    hidden_reduced_precision = hidden_state.astype(jnp.bfloat16)
    inner_hidden = jnp.einsum(
        "sjq,qy->sjy",
        hidden_reduced_precision,
        gathered_up_weight,
        preferred_element_type=jnp.float32,
    )
    gelu_activated = exact_gelu(inner_hidden).astype(jnp.bfloat16)
    residual_branch = jnp.einsum(
        "zya,av->zyv", gelu_activated, gathered_down_weight, preferred_element_type=jnp.float32
    )
    pre_two = hidden_state + residual_branch
    layer_output = layer_norm(
        pre_two, full_second_gain.astype(jnp.float32), full_second_shift.astype(jnp.float32)
    )
    again = (
        lax.all_gather(visual_matrix, "fsdp", axis=0, tiled=True),
        lax.all_gather(batch_gain, "fsdp", axis=0, tiled=True),
        lax.all_gather(attend_weight, "fsdp", axis=0, tiled=True),
        lax.all_gather(merge_weight, "fsdp", axis=0, tiled=True),
        lax.all_gather(first_gain, "fsdp", axis=0, tiled=True),
        lax.all_gather(up_matrix, "fsdp", axis=0, tiled=True),
        lax.all_gather(down_matrix, "fsdp", axis=0, tiled=True),
        lax.all_gather(second_gain, "fsdp", axis=0, tiled=True),
    )
    (
        visual_pullback,
        back_batch_gain,
        back_attend,
        back_merge,
        back_first_gain,
        up_pullback,
        down_pullback,
        back_second_gain,
    ) = again
    second_back = jax.vjp(
        layer_norm,
        pre_two,
        back_second_gain.astype(jnp.float32),
        full_second_shift.astype(jnp.float32),
    )[1]
    delta_two, second_gain_local, second_shift_local = second_back(cotangent.astype(jnp.float32))
    branch_gradient = delta_two.astype(jnp.bfloat16)
    down_local = jnp.einsum(
        "omt,oms->ts", gelu_activated, branch_gradient, preferred_element_type=jnp.float32
    )
    delta_activated = jnp.einsum(
        "ivj,hj->ivh", branch_gradient, down_pullback, preferred_element_type=jnp.float32
    )
    gelu_back = jax.vjp(exact_gelu, inner_hidden)[1]
    inner_gradient = gelu_back(delta_activated)[0].astype(jnp.bfloat16)
    up_local = jnp.einsum(
        "oih,oiu->hu", hidden_reduced_precision, inner_gradient, preferred_element_type=jnp.float32
    )
    delta_hidden = delta_two + jnp.einsum(
        "wmx,ix->wmi", inner_gradient, up_pullback, preferred_element_type=jnp.float32
    )
    first_back = jax.vjp(
        layer_norm,
        pre_one,
        back_first_gain.astype(jnp.float32),
        full_first_shift.astype(jnp.float32),
    )[1]
    delta_one, first_gain_local, first_shift_local = first_back(delta_hidden)
    delta_projected = delta_one.astype(jnp.bfloat16)
    merge_local = jnp.einsum(
        "drc,dre->ce", attended, delta_projected, preferred_element_type=jnp.float32
    )
    delta_attended = jnp.einsum(
        "dre,ce->drc", delta_projected, back_merge, preferred_element_type=jnp.float32
    ).astype(jnp.bfloat16)
    delta_packed = lax.map(attend_back, (packed, padding_mask, log_total, delta_attended))
    attend_local = jnp.einsum(
        "drc,dre->ce", joined_low, delta_packed, preferred_element_type=jnp.float32
    )
    delta_joined = delta_one + jnp.einsum(
        "dre,ce->drc", delta_packed, back_attend, preferred_element_type=jnp.float32
    )
    delta_embedded = jnp.einsum(
        "drs,drc->dsc",
        onehot_wide,
        delta_joined,
        precision=highest_precision,
        preferred_element_type=jnp.float32,
    )
    shift_total, gain_total = lax.psum(
        (jnp.sum(delta_embedded, axis=(0, 1)), jnp.sum(delta_embedded * normed, axis=(0, 1))),
        ("dp", "fsdp"),
    )
    visual_delta_rows = (
        valid_slot
        * back_batch_gain.astype(jnp.float32)
        * inverse_spread
        * (delta_embedded - shift_total / segment_total - normed * gain_total / segment_total)
    ).astype(jnp.bfloat16)
    visual_local = jnp.einsum(
        "bli,blz->iz", pooled_segments, visual_delta_rows, preferred_element_type=jnp.float32
    )
    delta_pooled = (
        jnp.einsum(
            "zbl,wl->zbw", visual_delta_rows, visual_pullback, preferred_element_type=jnp.float32
        )
        / divisor
    )
    text_gradient = delta_joined + jnp.einsum(
        "drs,dsc->drc",
        onehot_wide,
        delta_pooled,
        precision=highest_precision,
        preferred_element_type=jnp.float32,
    )
    (
        visual_shard,
        attend_shard,
        merge_shard,
        first_gain_shard,
        first_shift_shard,
        up_shard,
        down_shard,
        second_gain_shard,
        second_shift_shard,
    ) = (
        lax.psum_scatter(
            visual_local.astype(jnp.bfloat16), "fsdp", scatter_dimension=0, tiled=True
        ).astype(jnp.float32),
        lax.psum_scatter(
            attend_local.astype(jnp.bfloat16), "fsdp", scatter_dimension=0, tiled=True
        ).astype(jnp.float32),
        lax.psum_scatter(
            merge_local.astype(jnp.bfloat16), "fsdp", scatter_dimension=0, tiled=True
        ).astype(jnp.float32),
        lax.psum_scatter(
            first_gain_local.astype(jnp.bfloat16), "fsdp", scatter_dimension=0, tiled=True
        ).astype(jnp.float32),
        lax.psum_scatter(
            first_shift_local.astype(jnp.bfloat16), "fsdp", scatter_dimension=0, tiled=True
        ).astype(jnp.float32),
        lax.psum_scatter(
            up_local.astype(jnp.bfloat16), "fsdp", scatter_dimension=0, tiled=True
        ).astype(jnp.float32),
        lax.psum_scatter(
            down_local.astype(jnp.bfloat16), "fsdp", scatter_dimension=0, tiled=True
        ).astype(jnp.float32),
        lax.psum_scatter(
            second_gain_local.astype(jnp.bfloat16), "fsdp", scatter_dimension=0, tiled=True
        ).astype(jnp.float32),
        lax.psum_scatter(
            second_shift_local.astype(jnp.bfloat16), "fsdp", scatter_dimension=0, tiled=True
        ).astype(jnp.float32),
    )
    summed = (
        lax.psum(visual_shard.astype(jnp.bfloat16), "dp").astype(jnp.float32),
        lax.psum(attend_shard.astype(jnp.bfloat16), "dp").astype(jnp.float32),
        lax.psum(merge_shard.astype(jnp.bfloat16), "dp").astype(jnp.float32),
        lax.psum(first_gain_shard.astype(jnp.bfloat16), "dp").astype(jnp.float32),
        lax.psum(first_shift_shard.astype(jnp.bfloat16), "dp").astype(jnp.float32),
        lax.psum(up_shard.astype(jnp.bfloat16), "dp").astype(jnp.float32),
        lax.psum(down_shard.astype(jnp.bfloat16), "dp").astype(jnp.float32),
        lax.psum(second_gain_shard.astype(jnp.bfloat16), "dp").astype(jnp.float32),
        lax.psum(second_shift_shard.astype(jnp.bfloat16), "dp").astype(jnp.float32),
    )
    (
        visual_gradient,
        attend_gradient,
        merge_gradient,
        first_gain_gradient,
        first_shift_gradient,
        up_gradient,
        down_gradient,
        second_gain_gradient,
        second_shift_gradient,
    ) = summed
    piece = features // lax.axis_size("fsdp")
    start = lax.axis_index("fsdp") * piece
    batch_gain_gradient = lax.dynamic_slice_in_dim(gain_total, start, piece, 0)
    batch_shift_gradient = lax.dynamic_slice_in_dim(shift_total, start, piece, 0)
    return (
        layer_output,
        text_gradient,
        visual_gradient,
        batch_gain_gradient,
        batch_shift_gradient,
        attend_gradient,
        merge_gradient,
        first_gain_gradient,
        first_shift_gradient,
        up_gradient,
        down_gradient,
        second_gain_gradient,
        second_shift_gradient,
    )


def solution(mesh):
    in_specs = (
        P(("dp", "fsdp"), None, None),
        P("fsdp", None),
        P("fsdp"),
        P("fsdp"),
        P("fsdp", None),
        P("fsdp", None),
        P("fsdp"),
        P("fsdp"),
        P("fsdp", None),
        P("fsdp", None),
        P("fsdp"),
        P("fsdp"),
        P(("dp", "fsdp")),
        P(("dp", "fsdp"), None),
        P(("dp", "fsdp"), None),
        P(("dp", "fsdp"), None, None),
    )
    out_specs = (
        P(("dp", "fsdp"), None, None),
        P(("dp", "fsdp"), None, None),
        P("fsdp", None),
        P("fsdp"),
        P("fsdp"),
        P("fsdp", None),
        P("fsdp", None),
        P("fsdp"),
        P("fsdp"),
        P("fsdp", None),
        P("fsdp", None),
        P("fsdp"),
        P("fsdp"),
    )
    return jax.shard_map(shards, mesh=mesh, in_specs=in_specs, out_specs=out_specs, check_vma=False)
```

profile of v0, /device:TPU:0, one launch (start us, length us, event | category | flops | bytes accessed | tf_op | source)
XLA Modules:
  0.0 913.8 jit_solution(14838720792702939342)
XLA Ops:
  20.4 39.1 %all-reduce.13 = (bf16[768]{0:T(1024)(128)(2,1)S(1)}, bf16[768]{0:T(1024)(128)(2,1)S(1)}, bf16[768]{0:T(1024)(128)(2,1)S(1)}, bf16[768]{0:T(1024)(128)(2,1)S(1)}, bf16[768]{0:T(1024)(128)(2,1)S(1)}) all-reduce(bf16[768]{0:T(1024)(128)(2,1)S(1)} %dynamic-update-slice.1, ...), channel_id=1, replica_groups=mesh['dp'=4,'fsdp'=8] {'fsdp'}, use_global_device_ids=true, to_apply=%add.1 | all-reduce | flops 3840 | bytes 15360
  65.5 38.1 %all-reduce.11 = (f32[768]{0:T(1024)S(1)}, f32[]{:T(128)}) all-reduce(f32[768]{0:T(1024)S(1)} %get-tuple-element.172, f32[]{:T(128)S(6)} %convert_element_type.181), channel_id=1, replica_groups=mesh['dp'=4,'fsdp'=8] {'dp','fsdp'}, use_global_device_ids=true, to_apply=%region_2.0 | all-reduce | flops 769 | bytes 6152 | tf_op jit(solution)/shard_map/psum | solution.py:157
  104.5 42.7 %psum.100 = f32[768]{0:T(1024)S(1)} all-reduce(f32[768]{0:T(1024)S(1)} %fusion.53), channel_id=1, replica_groups=mesh['dp'=4,'fsdp'=8] {'dp','fsdp'}, use_global_device_ids=true, to_apply=%region_6.0 | all-reduce | flops 768 | bytes 6144 | tf_op jit(solution)/shard_map/psum | solution.py:163
  150.1 9.0 convolution_convert_fusion
  159.1 6.8 copy.50
  165.9 22.8 %while.22 = (s32[]{:T(128)}, bf16[2,512,768]{1,2,0:T(8,128)(2,1)S(1)}, f32[2,12,512]{2,1,0:T(8,128)S(1)}, bf16[2,512,2304]{1,2,0:T(8,128)(2,1)}, s32[2,512]{1,0:T(2,128)S(1)}, /*index=5*/s32[]{:T(128)}) while((s32[]{:T(128)}, bf16[2,512,768]{1,2,0:T(8,128)(2,1)S(1)}, f32[2,12,512]{2,1,0:T(8,128)S(1)}, bf16[2,512,2304]{1,2,0:T(8,128)(2,1)}, ...), condition=%wide.region_10.11_spmd, body=%wide.region_7.10_spmd.sunk | while | flops 843442688 | bytes 52129876 | solution.py:177
  189.9 4.8 fusion.77
  195.2 48.8 %all-gather.12.cloned.1.call-done = bf16[768,3072]{1,0:T(8,128)(2,1)} async-done(((bf16[96,3072]{1,0:T(8,128)(2,1)}), bf16[768,3072]{1,0:T(8,128)(2,1)}) %all-gather.12.cloned.1.call-update) | async-done | bytes 4718608 | tf_op jit(solution)/shard_map/all_gather | solution.py:124
  244.0 14.9 %fusion.36 = (u8[512,3072]{1,0:T(8,128)(4,1)S(1)}, u8[512,3072]{1,0:T(8,128)(4,1)S(1)}, f32[2,512,3072]{2,1,0:T(8,128)}) fusion(bf16[768,3072]{1,0:T(8,128)(2,1)} %all-gather.12.cloned.1.call-done, f32[2,512,768]{2,1,0:T(8,128)S(1)} %get-tuple-element.175, f32[768]{0:T(1024)S(1)} %copy-done.50, f32[768]{0:T(1024)S(1)} %copy-done.40, ...), kind=kOutput, calls=%fused_computation.80 | convolution fusion | flops 4873519104 | bytes 23607296 | tf_op jit(solution)/shard_map/sjq,qy->sjy/dot_general | solution.py:184
  258.9 31.0 %multiply_convert_fusion.3 = (bf16[2,512,3072]{2,1,0:T(8,128)(2,1)}, f32[2,512,3072]{2,1,0:T(8,128)}) fusion(f32[2,512,3072]{2,1,0:T(8,128)} %get-tuple-element.176, u8[512,3072]{1,0:T(8,128)(4,1)S(1)} %get-tuple-element.99, u8[512,3072]{1,0:T(8,128)(4,1)S(1)} %get-tuple-element.98), kind=kLoop, calls=%fused_computation.37 | loop fusion | flops 220200960 | bytes 34603008 | tf_op jit(solution)/shard_map/convert_element_type | solution.py:190
  289.9 34.1 %all-gather.14.cloned.1.call-done = bf16[3072,768]{1,0:T(8,128)(2,1)} async-done(((bf16[384,768]{1,0:T(8,128)(2,1)}), bf16[3072,768]{1,0:T(8,128)(2,1)}) %all-gather.14.cloned.1.call-update) | async-done | bytes 4718608 | tf_op jit(solution)/shard_map/all_gather | solution.py:125
  324.1 9.5 %fusion.78 = (f32[2,512]{1,0:T(2,128)S(1)}, f32[2,512,768]{2,1,0:T(8,128)S(1)}) fusion(bf16[2,512,3072]{2,1,0:T(8,128)(2,1)} %get-tuple-element.156, bf16[3072,768]{1,0:T(8,128)(2,1)} %all-gather.14.cloned.1.call-done, f32[768]{0:T(1024)S(1)} %copy-done.50, f32[768]{0:T(1024)S(1)} %copy-done.40, f32[2,512]{1,0:T(2,128)S(1)} %fusion.66, ...), kind=kOutput, calls=%fused_computation.142 | convolution fusion | flops 4836555776 | bytes 17319936 | tf_op jit(solution)/shard_map/zya,av->zyv/dot_general | solution.py:191
  337.1 16.4 %add_convert_fusion = bf16[2,512,3072]{2,1,0:T(8,128)(2,1)} fusion(f32[2,512,3072]{2,1,0:T(8,128)} %get-tuple-element.157, f32[2,512,3072]{2,1,0:T(8,128)} %get-tuple-element.176, bf16[3072,768]{1,0:T(8,128)(2,1)} %all-gather.14.cloned.1.call-done, f32[2,512]{1,0:T(2,128)S(1)} %negate_multiply_fusion.2, bf16[2,512,768]{2,1,0:T(8,128)(2,1)} %param.35, ...), kind=kOutput, calls=%fused_computation.36 | convolution fusion | flops 4882956288 | bytes 40913920 | tf_op jit(solution)/shard_map/ivj,hj->ivh/dot_general | solution.py:229
  353.5 11.2 %multiply_reduce_fusion.1 = (bf16[768]{0:T(1024)(128)(2,1)}, f32[2,512]{1,0:T(2,128)S(1)}, bf16[768]{0:T(1024)(128)(2,1)}, f32[2,512,768]{2,1,0:T(8,128)S(1)}) fusion(f32[2,512,768]{2,1,0:T(8,128)} %copy-done.2, f32[2,512]{1,0:T(2,128)S(1)} %fusion.66, f32[2,512]{1,0:T(2,128)S(1)} %broadcast_multiply_fusion.1, f32[768]{0:T(1024)S(1)} %copy-done.40, ...), kind=kOutput, calls=%fused_computation.72 | convolution fusion | flops 4845204480 | bytes 22057984 | tf_op jit(solution)/shard_map/wmx,ix->wmi/dot_general | solution.py:237
  372.6 77.6 %while.23 = (s32[]{:T(128)}, bf16[2,512,2304]{1,2,0:T(8,128)(2,1)}, bf16[2,512,2304]{1,2,0:T(8,128)(2,1)}, s32[2,512]{1,0:T(2,128)S(1)}, f32[2,12,512]{2,1,0:T(8...) while((s32[]{:T(128)}, bf16[2,512,2304]{1,2,0:T(8,128)(2,1)}, bf16[2,512,2304]{1,2,0:T(8,128)(2,1)}, ...), condition=%wide.region_21.22_spmd, body=%wide.region_19.21_spmd.sunk | while | flops 2069490176 | bytes 163754704 | solution.py:254
  375.1 6.4 fusion.145
  383.9 11.5 %multiply_reduce_fusion.8 = (f32[12,512]{1,0:T(8,128)S(1)}, f32[12,512,512]{1,2,0:T(8,128)}) fusion(f32[12,512,512]{1,2,0:T(8,128)} %fusion.145, f32[12,512]{1,0:T(8,128)S(1)} %dynamic-slice_bitcast_fusion.8, pred[512]{0:T(512)(128)(4,1)S(1)} %compare_reduce_fusion.5, bf16[512,12,64]{0,2,1:T(8,128)(2,1)S(1)} %bitcast.169, ...), kind=kOutput, calls=%fused_computation.14.clone.1 | convolution fusion | flops 418375680 | bytes 26788352 | tf_op jit(solution)/shard_map/while/body/eval_jaxpr/qhe,khe->hqk/dot_general | solution.py:67
  396.7 7.1 multiply_convert_fusion.8
  413.6 6.4 fusion.145
  422.4 11.5 %multiply_reduce_fusion.8 = (f32[12,512]{1,0:T(8,128)S(1)}, f32[12,512,512]{1,2,0:T(8,128)}) fusion(f32[12,512,512]{1,2,0:T(8,128)} %fusion.145, f32[12,512]{1,0:T(8,128)S(1)} %dynamic-slice_bitcast_fusion.8, pred[512]{0:T(512)(128)(4,1)S(1)} %compare_reduce_fusion.5, bf16[512,12,64]{0,2,1:T(8,128)(2,1)S(1)} %bitcast.169, ...), kind=kOutput, calls=%fused_computation.14.clone.1 | convolution fusion | flops 418375680 | bytes 26788352 | tf_op jit(solution)/shard_map/while/body/eval_jaxpr/qhe,khe->hqk/dot_general | solution.py:67
  435.1 7.1 multiply_convert_fusion.8
  450.3 8.5 add_add_fusion.2
  461.9 38.4 %all-reduce.10 = (f32[768]{0:T(1024)S(1)}, f32[768]{0:T(1024)S(1)}) all-reduce(f32[768]{0:T(1024)S(1)} %get-tuple-element.108, f32[768]{0:T(1024)S(1)} %get-tuple-element.107), channel_id=1, replica_groups=mesh['dp'=4,'fsdp'=8] {'dp','fsdp'}, use_global_device_ids=true, to_apply=%region_25.26 | all-reduce | flops 1536 | bytes 12288 | tf_op jit(solution)/shard_map/psum | solution.py:268
  505.0 8.5 bitcast_convert_fusion.2
  515.4 11.2 %bitcast_convert_fusion = bf16[3072,768]{1,0:T(8,128)(2,1)} fusion(bf16[2,512,3072]{2,1,0:T(8,128)(2,1)} %get-tuple-element.156, f32[2,512]{1,0:T(2,128)S(1)} %copy-done.53, bf16[2,512,768]{2,1,0:T(8,128)(2,1)} %param.35, f32[2,512,768]{2,1,0:T(8,128)S(1)} %copy-done.1, f32[2,512]{1,0:T(2,128)S(1)} %copy-done.46, f32[768]{0:T(1024)S(1)} %copy-done.27, ...), kind=kOutput, calls=%fused_computation.50 | convolution fusion | flops 4841275392 | bytes 15748096 | tf_op jit(solution)/shard_map/omt,oms->ts/dot_general | solution.py:226
  527.3 10.5 %bitcast_convert_fusion.1 = bf16[768,3072]{1,0:T(8,128)(2,1)} fusion(bf16[2,512,3072]{2,1,0:T(8,128)(2,1)} %add_convert_fusion, f32[2,512,768]{2,1,0:T(8,128)} %copy-done.2, f32[768]{0:T(1024)S(1)} %copy-done.51, f32[768]{0:T(1024)S(1)} %copy-done.41, f32[2,512]{1,0:T(2,128)S(1)} %copy-done.43, f32[2,512]{1,0:T(2,128)S(1)} %copy-done.37), kind=kOutput, calls=%fused_computation.51 | convolution fusion | flops 4838129664 | bytes 14170112 | tf_op jit(solution)/shard_map/oih,oiu->hu/dot_general | solution.py:234
  545.3 37.0 %all-reduce.12 = (bf16[768]{0:T(1024)(128)(2,1)}, bf16[768]{0:T(1024)(128)(2,1)}, bf16[768]{0:T(1024)(128)(2,1)}, bf16[768]{0:T(1024)(128)(2,1)}, bf16[768]{0:T(1024)(128)(2,1)}) all-reduce(bf16[768]{0:T(1024)(128)(2,1)} %dynamic-update-slice.5, bf16[768]{0:T(1024)(128)(2,1)} %get-tuple-element.100, ...), channel_id=1, replica_groups=mesh['dp'=4,'fsdp'=8] {'fsdp'}, use_global_device_ids=true, to_apply=%add.5 | all-reduce | flops 3840 | bytes 15360
  587.4 6.9 all-reduce.14
  600.3 50.8 %reduce-scatter.8.cloned.1.call-done = bf16[96,2304]{1,0:T(8,128)(2,1)} async-done(((bf16[768,2304]{1,0:T(8,128)(2,1)}), bf16[96,2304]{1,0:T(8,128)(2,1)}) %reduce-scatter.8.cloned.1.call-update) | async-done | bytes 442384 | tf_op jit(solution)/shard_map/reduce_scatter | solution.py:308
  651.0 98.7 %reduce-scatter.14.cloned.1.call-done = bf16[384,768]{1,0:T(8,128)(2,1)} async-done(((bf16[3072,768]{1,0:T(8,128)(2,1)}), bf16[384,768]{1,0:T(8,128)(2,1)}) %reduce-scatter.14.cloned.1.call-update) | async-done | bytes 589840 | tf_op jit(solution)/shard_map/reduce_scatter | solution.py:323
  749.7 98.5 %reduce-scatter.12.cloned.1.call-done = bf16[96,3072]{1,0:T(8,128)(2,1)} async-done(((bf16[768,3072]{1,0:T(8,128)(2,1)}), bf16[96,3072]{1,0:T(8,128)(2,1)}) %reduce-scatter.12.cloned.1.call-update) | async-done | bytes 589840 | tf_op jit(solution)/shard_map/reduce_scatter | solution.py:320
  856.2 44.0 %all-reduce.18.cloned.1.call-done = (bf16[96,768]{1,0:T(8,128)(2,1)}, bf16[96,2304]{1,0:T(8,128)(2,1)}, bf16[96,768]{1,0:T(8,128)(2,1)}, bf16[96,3072]{1,0:T(8,128)(2,1)}, bf16[384,768]{1,0:T(8,128)(2,1)}) async-done(((bf16[96,768]{1,0:T(8,128)(2,1)}, bf16[96,2304]{1,0:T(8,128)(2,1)}, bf16[96,768]{1,0:T(8,128)(2,1)}, bf16[96,3072]{1,0:T(8,128)(2,1)}, bf16[384,768]{1,0:T(8,128)(2,1)}), ...) | async-done | bytes 1916944 | tf_op jit(solution)/shard_map/psum | solution.py:334
  (263 shorter events, 126.3 us)
Async XLA Ops:
  7.2 56.3 %all-gather.6.cloned.1.call-start = ((), (), s32[]{:S(2)}) async-start(), calls=%async_computation.5 | async-start | bytes 1327104 | tf_op jit(solution)/shard_map/all_gather | solution.py:117
  7.9 142.2 %all-gather.8.cloned.1.call-start = ((), (), s32[]{:S(2)}) async-start(), calls=%async_computation.6 | async-start | bytes 3981312 | tf_op jit(solution)/shard_map/all_gather | solution.py:120
  8.7 180.1 %all-gather.10.cloned.1.call-start = ((), (), s32[]{:S(2)}) async-start(), calls=%async_computation.7 | async-start | bytes 1327104 | tf_op jit(solution)/shard_map/all_gather | solution.py:121
  9.4 234.6 %all-gather.12.cloned.1.call-start = ((), (), s32[]{:S(2)}) async-start(), calls=%async_computation.8 | async-start | bytes 5308416 | tf_op jit(solution)/shard_map/all_gather | solution.py:124
  10.0 314.1 %all-gather.14.cloned.1.call-start = ((), (), s32[]{:S(2)}) async-start(), calls=%async_computation.9 | async-start | bytes 5308416 | tf_op jit(solution)/shard_map/all_gather | solution.py:125
  10.6 589.7 %reduce-scatter.10.cloned.1.call-start = ((), (), s32[]{:S(2)}) async-start(), calls=%async_computation.12 | async-start | bytes 1327104 | tf_op jit(solution)/shard_map/reduce_scatter | solution.py:311
  11.4 92.9 %copy-start.47 = (f32[2,128]{1,0:T(2,128)}, f32[2,128]{1,0:T(2,128)S(1)}, u32[]{:S(2)}) copy-start(f32[2,128]{1,0:T(2,128)S(1)} %compare_convert_fusion) | copy-start | bytes 3076
  13.6 49.9 %copy-start.57 = (f32[2,128]{1,0:T(2,128)}, f32[2,128]{1,0:T(2,128)S(1)}, u32[]{:S(2)}) copy-start(f32[2,128]{1,0:T(2,128)S(1)} %broadcast_maximum_fusion) | copy-start | bytes 3076
  59.5 88.3 %copy-start.34 = (f32[768]{0:T(1024)}, f32[768]{0:T(1024)S(1)}, u32[]{:S(2)}) copy-start(f32[768]{0:T(1024)S(1)} %convert_element_type.182) | copy-start | bytes 9220
  61.3 86.5 %copy-start.30 = (s32[2,512]{1,0:T(2,128)S(1)}, s32[2,512]{1,0:T(2,128)}, u32[]{:S(2)}) copy-start(s32[2,512]{1,0:T(2,128)} %param.33) | copy-start | bytes 12292
  63.4 86.7 %copy-start.16 = (bf16[2,128,768]{2,1,0:T(8,128)(2,1)}, bf16[2,128,768]{2,1,0:T(8,128)(2,1)S(1)}, u32[]{:S(2)}) copy-start(bf16[2,128,768]{2,1,0:T(8,128)(2,1)S(1)} %fusion.47) | copy-start | bytes 1179652
  63.5 86.7 %copy-start.12 = (bf16[2,512,768]{2,1,0:T(8,128)(2,1)S(1)}, bf16[2,512,768]{2,1,0:T(8,128)(2,1)}, u32[]{:S(2)}) copy-start(bf16[2,512,768]{2,1,0:T(8,128)(2,1)} %param.20) | copy-start | bytes 4718596
  65.5 93.5 %copy-start.4 = (f32[2,128,768]{2,1,0:T(8,128)}, f32[2,128,768]{2,1,0:T(8,128)S(1)}, u32[]{:S(2)}) copy-start(f32[2,128,768]{2,1,0:T(8,128)S(1)} %get-tuple-element.173) | copy-start | bytes 2359300
  104.3 54.8 %copy-start.24 = (f32[768]{0:T(1024)}, f32[768]{0:T(1024)S(1)}, u32[]{:S(2)}) copy-start(f32[768]{0:T(1024)S(1)} %broadcast_divide_fusion.1) | copy-start | bytes 9220
  194.6 64.2 %copy-start.2 = (f32[2,512,768]{2,1,0:T(8,128)}, f32[2,512,768]{2,1,0:T(8,128)S(1)}, u32[]{:S(2)}) copy-start(f32[2,512,768]{2,1,0:T(8,128)S(1)} %get-tuple-element.175) | copy-start | bytes 9437188
  194.6 49.3 %copy-start.40 = (f32[768]{0:T(1024)S(1)}, f32[768]{0:T(1024)}, u32[]{:S(2)}) copy-start(f32[768]{0:T(1024)} %convert_element_type.187) | copy-start | bytes 9220
  194.7 49.3 %copy-start.50 = (f32[768]{0:T(1024)S(1)}, f32[768]{0:T(1024)}, u32[]{:S(2)}) copy-start(f32[768]{0:T(1024)} %convert_element_type.188) | copy-start | bytes 9220
  194.7 170.0 %copy-start.36 = (f32[2,512]{1,0:T(2,128)}, f32[2,512]{1,0:T(2,128)S(1)}, u32[]{:S(2)}) copy-start(f32[2,512]{1,0:T(2,128)S(1)} %broadcast_multiply_fusion.1) | copy-start | bytes 12292
  195.2 169.5 %copy-start.42 = (f32[2,512]{1,0:T(2,128)}, f32[2,512]{1,0:T(2,128)S(1)}, u32[]{:S(2)}) copy-start(f32[2,512]{1,0:T(2,128)S(1)} %fusion.66) | copy-start | bytes 12292
  333.6 19.8 %copy-start = (f32[2,512,768]{2,1,0:T(8,128)}, f32[2,512,768]{2,1,0:T(8,128)S(1)}, u32[]{:S(2)}) copy-start(f32[2,512,768]{2,1,0:T(8,128)S(1)} %get-tuple-element.178) | copy-start | bytes 9437188
  333.6 19.8 %copy-start.28 = (f32[2,512]{1,0:T(2,128)}, f32[2,512]{1,0:T(2,128)S(1)}, u32[]{:S(2)}) copy-start(f32[2,512]{1,0:T(2,128)S(1)} %broadcast_multiply_fusion) | copy-start | bytes 12292
  334.7 18.8 %copy-start.38 = (f32[2,512]{1,0:T(2,128)}, f32[2,512]{1,0:T(2,128)S(1)}, u32[]{:S(2)}) copy-start(f32[2,512]{1,0:T(2,128)S(1)} %get-tuple-element.169) | copy-start | bytes 12292
  368.7 231.6 %reduce-scatter.6.cloned.1.call-start = ((), (), s32[]{:S(2)}) async-start(), calls=%async_computation.10 | async-start | bytes 1327104 | tf_op jit(solution)/shard_map/reduce_scatter | solution.py:305
  372.6 77.6 %copy-start.56 = (f32[2,512]{1,0:T(2,128)S(1)}, f32[2,512]{1,0:T(2,128)}, u32[]{:S(2)}) copy-start(f32[2,512]{1,0:T(2,128)} %copy-done.55) | copy-start | bytes 12292
  460.4 40.6 %copy-start.35 = (f32[768]{0:T(1024)S(1)}, f32[768]{0:T(1024)}, u32[]{:S(2)}) copy-start(f32[768]{0:T(1024)} %copy-done.34) | copy-start | bytes 9220
  460.4 40.6 %copy-start.48 = (f32[2,128]{1,0:T(2,128)S(1)}, f32[2,128]{1,0:T(2,128)}, u32[]{:S(2)}) copy-start(f32[2,128]{1,0:T(2,128)} %copy-done.47) | copy-start | bytes 3076
  460.4 42.3 %copy-start.17 = (bf16[2,128,768]{2,1,0:T(8,128)(2,1)S(1)}, bf16[2,128,768]{2,1,0:T(8,128)(2,1)}, u32[]{:S(2)}) copy-start(bf16[2,128,768]{2,1,0:T(8,128)(2,1)} %copy-done.16) | copy-start | bytes 1179652
  504.3 146.8 %reduce-scatter.8.cloned.1.call-start = ((), (), s32[]{:S(2)}) async-start(), calls=%async_computation.11 | async-start | bytes 3981312 | tf_op jit(solution)/shard_map/reduce_scatter | solution.py:308
  513.6 236.1 %reduce-scatter.14.cloned.1.call-start = ((), (), s32[]{:S(2)}) async-start(), calls=%async_computation.14 | async-start | bytes 5308416 | tf_op jit(solution)/shard_map/reduce_scatter | solution.py:323
  526.6 321.6 %reduce-scatter.12.cloned.1.call-start = ((), (), s32[]{:S(2)}) async-start(), calls=%async_computation.13 | async-start | bytes 5308416 | tf_op jit(solution)/shard_map/reduce_scatter | solution.py:320
  537.8 310.5 %copy-start.19 = (bf16[2,128,768]{2,1,0:T(8,128)(2,1)S(1)}, bf16[2,128,768]{2,1,0:T(8,128)(2,1)}, u32[]{:S(2)}) copy-start(bf16[2,128,768]{2,1,0:T(8,128)(2,1)} %copy-done.18) | copy-start | bytes 1179652
  537.8 362.3 %all-reduce.18.cloned.1.call-start = ((), (), s32[]{:S(2)}) async-start(), calls=%async_computation.15 | async-start | bytes 3833856 | tf_op jit(solution)/shard_map/psum | solution.py:334
  (44 other events, 264.4 us)
Sparse Core Ops, SparseCore 0:
  10.2 44.0 all-gather.5
  56.5 64.8 all-gather.7
  123.5 39.6 all-gather.9
  165.3 78.6 all-gather.11
  246.0 78.0 all-gather.13
  368.8 62.2 reduce-scatter.9
  504.4 64.7 reduce-scatter.5
  572.9 78.1 reduce-scatter.7
  654.7 94.9 reduce-scatter.13
  753.2 95.0 reduce-scatter.11
  851.0 49.1 all-reduce.17
where the time goes:
time: 922 us; the launch traced here: 914 us
  waiting for transfers between devices  378 us (41%)
  blocking collectives  202 us (22%)
  matrix products  186 us (20%)
  other arithmetic  84 us (9%)
  local copies, waits for them, and re-layouts  44.5 us (5%)
  between operations  16.8 us (2%)
    reduce_scatter x1, waiting for transfers between devices, shards(): lax.psum_scatter(down_local.astype(jnp.bfloat16), 'fsdp', scatter_dimensi...  98.7 us
    reduce_scatter x1, waiting for transfers between devices, shards(): lax.psum_scatter(up_local.astype(jnp.bfloat16), 'fsdp', scatter_dimension...  98.5 us
    unnamed x2, blocking collectives  76.1 us
    reduce_scatter x1, waiting for transfers between devices, shards(): lax.psum_scatter(attend_local.astype(jnp.bfloat16), 'fsdp', scatter_dimen...  50.8 us
    all_gather x1, waiting for transfers between devices, shards(): lax.all_gather(up_matrix, 'fsdp', axis=0, tiled=True)  48.8 us
    psum x1, waiting for transfers between devices, shards(): lax.psum(visual_shard.astype(jnp.bfloat16), 'dp').astype(jnp.float32)  44 us
    psum x1, blocking collectives, shards(): lax.psum(jnp.sum(valid_slot * center * center, axis=(0, 1)), ('dp', 'fsdp'))  42.7 us
    psum x1, blocking collectives, shards(): lax.psum((jnp.sum(delta_embedded, axis=(0, 1)), jnp.sum(delta_embedded *...  38.4 us
  transfers between devices with their start and end apart: 11, of which 6 were waited for; matrix products, arithmetic and copies ran while one was open for 28% of the time, Pallas kernels for 0%

commit v1 on v0

--- a/solution.py
+++ b/solution.py
@@ -9,6 +9,19 @@
 eps_batch = 1e-05
 masked_score = -1e30
 highest_precision = lax.Precision.HIGHEST
+
+
+def ring_gather(shard, axis, dim):
+    size, index, rows = (lax.axis_size(axis), lax.axis_index(axis), shard.shape[dim])
+    upward = [(i, (i + 1) % size) for i in range(size)]
+    out = jnp.zeros((*shard.shape[:dim], size * rows, *shard.shape[dim + 1 :]), shard.dtype)
+    held = shard
+    for step in range(size):
+        holder = (index - step) % size
+        out = lax.dynamic_update_slice_in_dim(out, held, holder * rows, axis=dim)
+        if step < size - 1:
+            held = lax.ppermute(held, axis, upward)
+    return out
 
 
 def layer_norm(values, gain, shift):
@@ -121,7 +134,7 @@
         lax.all_gather(merge_weight, "fsdp", axis=0, tiled=True),
         lax.all_gather(first_gain, "fsdp", axis=0, tiled=True),
         lax.all_gather(first_shift, "fsdp", axis=0, tiled=True),
-        lax.all_gather(up_matrix, "fsdp", axis=0, tiled=True),
+        ring_gather(up_matrix, "fsdp", 0),
         lax.all_gather(down_matrix, "fsdp", axis=0, tiled=True),
         lax.all_gather(second_gain, "fsdp", axis=0, tiled=True),
         lax.all_gather(second_shift, "fsdp", axis=0, tiled=True),

time: 922 us -> 973 us (1.055)
  blocking collectives: 202 us -> 235 us
    ppermute x0 -> x7, waiting for transfers between devices: none -> 83.5 us  [ring_gather(): held = lax.ppermute(held, axis, upward)]
    all_gather x1, waiting for transfers between devices: 48.8 us -> 0.01 us  [shards(): lax.all_gather(up_matrix, 'fsdp', axis=0, tiled=True)]
    all_gather x1, waiting for transfers between devices: 34.1 us -> 0.02 us  [shards(): lax.all_gather(down_matrix, 'fsdp', axis=0, tiled=True)]
    psum x1, blocking collectives: 38.1 us -> 55.3 us  [shards(): lax.psum((local_count, jnp.sum(masked_visual, axis=(0, 1))), ('dp', 'fsdp'))]
    unnamed x131 -> x137, local copies, waits for them, and re-layouts: 19.9 us -> 14.2 us
  transfers between devices with their start and end apart: 11 -> 18, of which waited for: 6 -> 8; matrix products, arithmetic and copies ran while one was open for 28% -> 30% of each run, Pallas kernels for 0% -> 0%
where the time goes in v1:
time: 973 us; the launch traced here: 965 us
  waiting for transfers between devices  378 us (39%)
  blocking collectives  235 us (24%)
  matrix products  188 us (19%)
  other arithmetic  85.2 us (9%)
  local copies, waits for them, and re-layouts  50.8 us (5%)
  between operations  17.1 us (2%)
    reduce_scatter x1, waiting for transfers between devices, shards(): lax.psum_scatter(up_local.astype(jnp.bfloat16), 'fsdp', scatter_dimension...  98.5 us
    reduce_scatter x1, waiting for transfers between devices, shards(): lax.psum_scatter(down_local.astype(jnp.bfloat16), 'fsdp', scatter_dimensi...  98.5 us
    ppermute x7, waiting for transfers between devices, ring_gather(): held = lax.ppermute(held, axis, upward)  83.5 us
    unnamed x2, blocking collectives  78.7 us
    psum x1, blocking collectives, shards(): lax.psum((local_count, jnp.sum(masked_visual, axis=(0, 1))), ('dp', 'fsdp'))  55.3 us
    reduce_scatter x1, waiting for transfers between devices, shards(): lax.psum_scatter(attend_local.astype(jnp.bfloat16), 'fsdp', scatter_dimen...  50.9 us
    psum x1, blocking collectives, shards(): lax.psum(jnp.sum(valid_slot * center * center, axis=(0, 1)), ('dp', 'fsdp'))  47.5 us
    psum x1, blocking collectives, shards(): lax.psum((jnp.sum(delta_embedded, axis=(0, 1)), jnp.sum(delta_embedded *...  46.9 us
  transfers between devices with their start and end apart: 18, of which 8 were waited for; matrix products, arithmetic and copies ran while one was open for 30% of the time, Pallas kernels for 0%

profile of v1, /device:TPU:0, one launch (start us, length us, event | category | flops | bytes accessed | tf_op | source)
XLA Modules:
  0.0 964.6 jit_solution(13696947852927896498)
XLA Ops:
  14.1 19.1 %collective-permute-done = bf16[96,3072]{1,0:T(8,128)(2,1)S(1)} collective-permute-done((bf16[96,3072]{1,0:T(8,128)(2,1)}, bf16[96,3072]{1,0:T(8,128)(2,1)S(1)}, u32[]{:S(2)}, u32[]{:S(2)}) %collective-permute-start) | collective-permute-done | bytes 589856 | tf_op jit(solution)/shard_map/ppermute | solution.py:23
  39.3 41.4 %all-reduce.13 = (bf16[768]{0:T(1024)(128)(2,1)S(1)}, bf16[768]{0:T(1024)(128)(2,1)S(1)}, bf16[768]{0:T(1024)(128)(2,1)S(1)}, bf16[768]{0:T(1024)(128)(2,1)S(1)}, bf16[768]{0:T(1024)(128)(2,1)S(1)}) all-reduce(bf16[768]{0:T(1024)(128)(2,1)S(1)} %dynamic-update-slice.1, ...), channel_id=1, replica_groups=mesh['dp'=4,'fsdp'=8] {'fsdp'}, use_global_device_ids=true, to_apply=%add.1 | all-reduce | flops 3840 | bytes 15360
  88.7 14.5 %collective-permute-done.2 = bf16[96,3072]{1,0:T(8,128)(2,1)S(1)} collective-permute-done((bf16[96,3072]{1,0:T(8,128)(2,1)S(1)}, bf16[96,3072]{1,0:T(8,128)(2,1)S(1)}, u32[]{:S(2)}, u32[]{:S(2)}) %collective-permute-start.2) | collective-permute-done | bytes 589856 | tf_op jit(solution)/shard_map/ppermute | solution.py:23
  105.9 55.3 %all-reduce.11 = (f32[768]{0:T(1024)S(1)}, f32[]{:T(128)}) all-reduce(f32[768]{0:T(1024)S(1)} %get-tuple-element.172, f32[]{:T(128)S(6)} %convert_element_type.181), channel_id=1, replica_groups=mesh['dp'=4,'fsdp'=8] {'dp','fsdp'}, use_global_device_ids=true, to_apply=%region_2.3 | all-reduce | flops 769 | bytes 6152 | tf_op jit(solution)/shard_map/psum | solution.py:170
  165.2 47.5 %psum.100 = f32[768]{0:T(1024)S(1)} all-reduce(f32[768]{0:T(1024)S(1)} %fusion.53), channel_id=1, replica_groups=mesh['dp'=4,'fsdp'=8] {'dp','fsdp'}, use_global_device_ids=true, to_apply=%region_6.7 | all-reduce | flops 768 | bytes 6144 | tf_op jit(solution)/shard_map/psum | solution.py:176
  218.8 20.4 %collective-permute-done.5 = bf16[96,3072]{1,0:T(8,128)(2,1)S(1)} collective-permute-done((bf16[96,3072]{1,0:T(8,128)(2,1)S(1)}, bf16[96,3072]{1,0:T(8,128)(2,1)S(1)}, u32[]{:S(2)}, u32[]{:S(2)}) %collective-permute-start.5) | collective-permute-done | bytes 589856 | tf_op jit(solution)/shard_map/ppermute | solution.py:23
  241.0 29.4 %collective-permute-done.6 = bf16[96,3072]{1,0:T(8,128)(2,1)S(1)} collective-permute-done((bf16[96,3072]{1,0:T(8,128)(2,1)S(1)}, bf16[96,3072]{1,0:T(8,128)(2,1)S(1)}, u32[]{:S(2)}, u32[]{:S(2)}) %collective-permute-start.6) | collective-permute-done | bytes 589856 | tf_op jit(solution)/shard_map/ppermute | solution.py:23
  271.2 9.0 convolution_convert_fusion
  280.2 7.2 copy.50
  287.4 24.2 %while.22 = (s32[]{:T(128)}, bf16[2,512,768]{1,2,0:T(8,128)(2,1)}, f32[2,12,512]{2,1,0:T(8,128)S(1)}, bf16[2,512,2304]{1,2,0:T(8,128)(2,1)}, s32[2,512]{1,0:T(2,128)S(1)}, /*index=5*/s32[]{:T(128)}) while((s32[]{:T(128)}, bf16[2,512,768]{1,2,0:T(8,128)(2,1)}, f32[2,12,512]{2,1,0:T(8,128)S(1)}, bf16[2,512,2304]{1,2,0:T(8,128)(2,1)}, ...), condition=%wide.region_10.11_spmd, body=%wide.region_7.10_spmd.sunk | while | flops 843442688 | bytes 52130384 | solution.py:190
  316.1 15.0 %fusion.36 = (u8[512,3072]{1,0:T(8,128)(4,1)S(1)}, u8[512,3072]{1,0:T(8,128)(4,1)S(1)}, f32[2,512,3072]{2,1,0:T(8,128)}) fusion(bf16[768,3072]{1,0:T(8,128)(2,1)} %constant_dynamic-update-slice_fusion.1, f32[2,512,768]{2,1,0:T(8,128)S(1)} %get-tuple-element.175, f32[768]{0:T(1024)S(1)} %copy-done.47, f32[768]{0:T(1024)S(1)} %copy-done.40, ...), kind=kOutput, calls=%fused_computation.80 | convolution fusion | flops 4873519104 | bytes 23607296 | tf_op jit(solution)/shard_map/sjq,qy->sjy/dot_general | solution.py:197
  331.0 31.1 %multiply_convert_fusion.3 = (bf16[2,512,3072]{2,1,0:T(8,128)(2,1)}, f32[2,512,3072]{2,1,0:T(8,128)}) fusion(f32[2,512,3072]{2,1,0:T(8,128)} %get-tuple-element.176, u8[512,3072]{1,0:T(8,128)(4,1)S(1)} %get-tuple-element.99, u8[512,3072]{1,0:T(8,128)(4,1)S(1)} %get-tuple-element.98), kind=kLoop, calls=%fused_computation.37 | loop fusion | flops 220200960 | bytes 34603008 | tf_op jit(solution)/shard_map/convert_element_type | solution.py:203
  362.2 9.5 fusion.78
  375.2 16.4 %add_convert_fusion = bf16[2,512,3072]{2,1,0:T(8,128)(2,1)} fusion(f32[2,512,3072]{2,1,0:T(8,128)} %get-tuple-element.157, f32[2,512,3072]{2,1,0:T(8,128)} %get-tuple-element.176, bf16[3072,768]{1,0:T(8,128)(2,1)} %all-gather.12.cloned.1.call-done, f32[2,512]{1,0:T(2,128)S(1)} %negate_multiply_fusion.2, bf16[2,512,768]{2,1,0:T(8,128)(2,1)} %param.35, ...), kind=kOutput, calls=%fused_computation.36 | convolution fusion | flops 4882956288 | bytes 40913920 | tf_op jit(solution)/shard_map/ivj,hj->ivh/dot_general | solution.py:242
  391.6 11.2 %multiply_reduce_fusion.1 = (bf16[768]{0:T(1024)(128)(2,1)}, f32[2,512]{1,0:T(2,128)S(1)}, bf16[768]{0:T(1024)(128)(2,1)}, f32[2,512,768]{2,1,0:T(8,128)S(1)}) fusion(f32[2,512,768]{2,1,0:T(8,128)} %copy-done.2, f32[2,512]{1,0:T(2,128)S(1)} %fusion.66, f32[2,512]{1,0:T(2,128)S(1)} %broadcast_multiply_fusion.1, f32[768]{0:T(1024)S(1)} %copy-done.40, ...), kind=kOutput, calls=%fused_computation.72 | convolution fusion | flops 4845204480 | bytes 22057984 | tf_op jit(solution)/shard_map/wmx,ix->wmi/dot_general | solution.py:250
  413.2 77.4 %while.23 = (s32[]{:T(128)}, bf16[2,512,2304]{1,2,0:T(8,128)(2,1)}, bf16[2,512,2304]{1,2,0:T(8,128)(2,1)}, s32[2,512]{1,0:T(2,128)S(1)}, f32[2,12,512]{2,1,0:T(8...) while((s32[]{:T(128)}, bf16[2,512,2304]{1,2,0:T(8,128)(2,1)}, bf16[2,512,2304]{1,2,0:T(8,128)(2,1)}, ...), condition=%wide.region_21.22_spmd, body=%wide.region_19.21_spmd.sunk | while | flops 2069490176 | bytes 163754704 | solution.py:267
  424.4 11.5 %multiply_reduce_fusion.8 = (f32[12,512]{1,0:T(8,128)S(1)}, f32[12,512,512]{1,2,0:T(8,128)}) fusion(f32[12,512,512]{1,2,0:T(8,128)} %fusion.145, f32[12,512]{1,0:T(8,128)S(1)} %dynamic-slice_bitcast_fusion.8, pred[512]{0:T(512)(128)(4,1)S(1)} %compare_reduce_fusion.5, bf16[512,12,64]{0,2,1:T(8,128)(2,1)S(1)} %bitcast.170, ...), kind=kOutput, calls=%fused_computation.14.clone.1 | convolution fusion | flops 418375680 | bytes 26788352 | tf_op jit(solution)/shard_map/while/body/eval_jaxpr/qhe,khe->hqk/dot_general | solution.py:80
  437.1 7.1 multiply_convert_fusion.8
  453.9 6.4 fusion.145
  462.7 11.5 %multiply_reduce_fusion.8 = (f32[12,512]{1,0:T(8,128)S(1)}, f32[12,512,512]{1,2,0:T(8,128)}) fusion(f32[12,512,512]{1,2,0:T(8,128)} %fusion.145, f32[12,512]{1,0:T(8,128)S(1)} %dynamic-slice_bitcast_fusion.8, pred[512]{0:T(512)(128)(4,1)S(1)} %compare_reduce_fusion.5, bf16[512,12,64]{0,2,1:T(8,128)(2,1)S(1)} %bitcast.170, ...), kind=kOutput, calls=%fused_computation.14.clone.1 | convolution fusion | flops 418375680 | bytes 26788352 | tf_op jit(solution)/shard_map/while/body/eval_jaxpr/qhe,khe->hqk/dot_general | solution.py:80
  475.5 7.2 multiply_convert_fusion.8
  490.6 8.5 add_add_fusion.2
  502.9 46.9 %all-reduce.10 = (f32[768]{0:T(1024)}, f32[768]{0:T(1024)}) all-reduce(f32[768]{0:T(1024)} %get-tuple-element.108, f32[768]{0:T(1024)} %get-tuple-element.107), channel_id=1, replica_groups=mesh['dp'=4,'fsdp'=8] {'dp','fsdp'}, use_global_device_ids=true, to_apply=%region_25.26 | all-reduce | flops 1536 | bytes 12288 | tf_op jit(solution)/shard_map/psum | solution.py:281
  555.1 9.0 bitcast_convert_fusion.2
  566.1 11.1 %bitcast_convert_fusion = bf16[3072,768]{1,0:T(8,128)(2,1)} fusion(bf16[2,512,3072]{2,1,0:T(8,128)(2,1)} %get-tuple-element.156, f32[2,512]{1,0:T(2,128)S(1)} %copy-done.50, bf16[2,512,768]{2,1,0:T(8,128)(2,1)} %param.35, f32[2,512,768]{2,1,0:T(8,128)S(1)} %copy-done.1, f32[2,512]{1,0:T(2,128)S(1)} %copy-done.46, f32[768]{0:T(1024)S(1)} %copy-done.27, ...), kind=kOutput, calls=%fused_computation.50 | convolution fusion | flops 4841275392 | bytes 15748096 | tf_op jit(solution)/shard_map/omt,oms->ts/dot_general | solution.py:239
  578.0 10.5 %bitcast_convert_fusion.1 = bf16[768,3072]{1,0:T(8,128)(2,1)} fusion(bf16[2,512,3072]{2,1,0:T(8,128)(2,1)} %add_convert_fusion, f32[2,512,768]{2,1,0:T(8,128)} %copy-done.2, f32[768]{0:T(1024)S(1)} %copy-done.48, f32[768]{0:T(1024)S(1)} %copy-done.41, f32[2,512]{1,0:T(2,128)S(1)} %copy-done.43, f32[2,512]{1,0:T(2,128)S(1)} %copy-done.37), kind=kOutput, calls=%fused_computation.51 | convolution fusion | flops 4838129664 | bytes 14170112 | tf_op jit(solution)/shard_map/oih,oiu->hu/dot_general | solution.py:247
  595.9 37.3 %all-reduce.12 = (bf16[768]{0:T(1024)(128)(2,1)}, bf16[768]{0:T(1024)(128)(2,1)}, bf16[768]{0:T(1024)(128)(2,1)}, bf16[768]{0:T(1024)(128)(2,1)}, bf16[768]{0:T(1024)(128)(2,1)}) all-reduce(bf16[768]{0:T(1024)(128)(2,1)} %dynamic-update-slice.5, bf16[768]{0:T(1024)(128)(2,1)} %get-tuple-element.100, ...), channel_id=1, replica_groups=mesh['dp'=4,'fsdp'=8] {'fsdp'}, use_global_device_ids=true, to_apply=%add.5 | all-reduce | flops 3840 | bytes 15360
  638.3 6.9 all-reduce.14
  651.2 50.9 %reduce-scatter.8.cloned.1.call-done = bf16[96,2304]{1,0:T(8,128)(2,1)} async-done(((bf16[768,2304]{1,0:T(8,128)(2,1)}), bf16[96,2304]{1,0:T(8,128)(2,1)}) %reduce-scatter.8.cloned.1.call-update) | async-done | bytes 442384 | tf_op jit(solution)/shard_map/reduce_scatter | solution.py:321
  702.0 98.5 %reduce-scatter.14.cloned.1.call-done = bf16[384,768]{1,0:T(8,128)(2,1)} async-done(((bf16[3072,768]{1,0:T(8,128)(2,1)}), bf16[384,768]{1,0:T(8,128)(2,1)}) %reduce-scatter.14.cloned.1.call-update) | async-done | bytes 589840 | tf_op jit(solution)/shard_map/reduce_scatter | solution.py:336
  800.6 98.5 %reduce-scatter.12.cloned.1.call-done = bf16[96,3072]{1,0:T(8,128)(2,1)} async-done(((bf16[768,3072]{1,0:T(8,128)(2,1)}), bf16[96,3072]{1,0:T(8,128)(2,1)}) %reduce-scatter.12.cloned.1.call-update) | async-done | bytes 589840 | tf_op jit(solution)/shard_map/reduce_scatter | solution.py:333
  907.0 44.0 %all-reduce.18.cloned.1.call-done = (bf16[96,768]{1,0:T(8,128)(2,1)}, bf16[96,2304]{1,0:T(8,128)(2,1)}, bf16[96,768]{1,0:T(8,128)(2,1)}, bf16[96,3072]{1,0:T(8,128)(2,1)}, bf16[384,768]{1,0:T(8,128)(2,1)}) async-done(((bf16[96,768]{1,0:T(8,128)(2,1)}, bf16[96,2304]{1,0:T(8,128)(2,1)}, bf16[96,768]{1,0:T(8,128)(2,1)}, bf16[96,3072]{1,0:T(8,128)(2,1)}, bf16[384,768]{1,0:T(8,128)(2,1)}), ...) | async-done | bytes 1916944 | tf_op jit(solution)/shard_map/psum | solution.py:347
  (292 shorter events, 153.9 us)
Async XLA Ops:
  7.3 96.9 %all-gather.6.cloned.1.call-start = ((), (), s32[]{:S(2)}) async-start(), calls=%async_computation.5 | async-start | bytes 1327104 | tf_op jit(solution)/shard_map/all_gather | solution.py:130
  8.0 263.2 %all-gather.8.cloned.1.call-start = ((), (), s32[]{:S(2)}) async-start(), calls=%async_computation.6 | async-start | bytes 3981312 | tf_op jit(solution)/shard_map/all_gather | solution.py:133
  8.7 302.9 %all-gather.10.cloned.1.call-start = ((), (), s32[]{:S(2)}) async-start(), calls=%async_computation.7 | async-start | bytes 1327104 | tf_op jit(solution)/shard_map/all_gather | solution.py:134
  9.5 352.7 %all-gather.12.cloned.1.call-start = ((), (), s32[]{:S(2)}) async-start(), calls=%async_computation.8 | async-start | bytes 5308416 | tf_op jit(solution)/shard_map/all_gather | solution.py:138
  10.0 381.5 %all-gather.14.cloned.1.call-start = ((), (), s32[]{:S(2)}) async-start(), calls=%async_computation.9 | async-start | bytes 5308416 | tf_op jit(solution)/shard_map/all_gather | solution.py:217
  10.1 23.2 %collective-permute-start = (bf16[96,3072]{1,0:T(8,128)(2,1)}, bf16[96,3072]{1,0:T(8,128)(2,1)S(1)}, u32[]{:S(2)}, u32[]{:S(2)}) collective-permute-start(bf16[96,3072]{1,0:T(8,128)(2,1)} %param.28), channel_id=1, source_target_pairs={{0,1},{1,2},{2,3},{3,4},{4,5},{5,6},{6,7},{7,0},{8,9},{9,10},{10,1... | collective-permute-start | bytes 1769480 | tf_op jit(solution)/shard_map/ppermute | solution.py:23
  13.1 638.0 %reduce-scatter.10.cloned.1.call-start = ((), (), s32[]{:S(2)}) async-start(), calls=%async_computation.12 | async-start | bytes 1327104 | tf_op jit(solution)/shard_map/reduce_scatter | solution.py:324
  33.3 53.4 %collective-permute-start.1 = (bf16[96,3072]{1,0:T(8,128)(2,1)S(1)}, bf16[96,3072]{1,0:T(8,128)(2,1)S(1)}, u32[]{:S(2)}, u32[]{:S(2)}) collective-permute-start(bf16[96,3072]{1,0:T(8,128)(2,1)S(1)} %collective-permute-done), channel_id=1, source_target_pairs={{0,1},{1,2},{2,3},{3,4},{4,5},{5,6},{6,7},{7,0},{8,9},{9,10},{10,1... | collective-permute-start | bytes 1769480 | tf_op jit(solution)/shard_map/ppermute | solution.py:23
  35.3 68.8 %copy-start.15 = (bf16[2,128,768]{2,1,0:T(8,128)(2,1)}, bf16[2,128,768]{2,1,0:T(8,128)(2,1)S(1)}, u32[]{:S(2)}) copy-start(bf16[2,128,768]{2,1,0:T(8,128)(2,1)S(1)} %fusion.47) | copy-start | bytes 1179652
  35.3 50.4 %copy-start.12 = (bf16[96,3072]{1,0:T(8,128)(2,1)S(1)}, bf16[96,3072]{1,0:T(8,128)(2,1)}, u32[]{:S(2)}) copy-start(bf16[96,3072]{1,0:T(8,128)(2,1)} %param.28) | copy-start | bytes 1769476
  80.7 135.0 %copy-start.34 = (f32[768]{0:T(1024)}, f32[768]{0:T(1024)S(1)}, u32[]{:S(2)}) copy-start(f32[768]{0:T(1024)S(1)} %convert_element_type.182) | copy-start | bytes 9220
  86.6 129.0 %copy-start.30 = (s32[2,512]{1,0:T(2,128)S(1)}, s32[2,512]{1,0:T(2,128)}, u32[]{:S(2)}) copy-start(s32[2,512]{1,0:T(2,128)} %param.33) | copy-start | bytes 12292
  86.6 16.6 %collective-permute-start.2 = (bf16[96,3072]{1,0:T(8,128)(2,1)S(1)}, bf16[96,3072]{1,0:T(8,128)(2,1)S(1)}, u32[]{:S(2)}, u32[]{:S(2)}) collective-permute-start(bf16[96,3072]{1,0:T(8,128)(2,1)S(1)} %collective-permute-done.1), channel_id=1, source_target_pairs={{0,1},{1,2},{2,3},{3,4},{4,5},{5,6},{6,7},{7,0},{8,9},{9,10},{10,1... | collective-permute-start | bytes 1769480 | tf_op jit(solution)/shard_map/ppermute | solution.py:23
  103.2 58.0 %collective-permute-start.3 = (bf16[96,3072]{1,0:T(8,128)(2,1)S(1)}, bf16[96,3072]{1,0:T(8,128)(2,1)S(1)}, u32[]{:S(2)}, u32[]{:S(2)}) collective-permute-start(bf16[96,3072]{1,0:T(8,128)(2,1)S(1)} %collective-permute-done.2), channel_id=1, source_target_pairs={{0,1},{1,2},{2,3},{3,4},{4,5},{5,6},{6,7},{7,0},{8,9},{9,10},{10,1... | collective-permute-start | bytes 1769480 | tf_op jit(solution)/shard_map/ppermute | solution.py:23
  105.9 134.3 %copy-start.4 = (f32[2,128,768]{2,1,0:T(8,128)}, f32[2,128,768]{2,1,0:T(8,128)S(1)}, u32[]{:S(2)}) copy-start(f32[2,128,768]{2,1,0:T(8,128)S(1)} %get-tuple-element.173) | copy-start | bytes 2359300
  161.2 52.1 %collective-permute-start.4 = (bf16[96,3072]{1,0:T(8,128)(2,1)S(1)}, bf16[96,3072]{1,0:T(8,128)(2,1)S(1)}, u32[]{:S(2)}, u32[]{:S(2)}) collective-permute-start(bf16[96,3072]{1,0:T(8,128)(2,1)S(1)} %collective-permute-done.3), channel_id=1, source_target_pairs={{0,1},{1,2},{2,3},{3,4},{4,5},{5,6},{6,7},{7,0},{8,9},{9,10},{10,1... | collective-permute-start | bytes 1769480 | tf_op jit(solution)/shard_map/ppermute | solution.py:23
  164.4 75.8 %copy-start.24 = (f32[768]{0:T(1024)}, f32[768]{0:T(1024)S(1)}, u32[]{:S(2)}) copy-start(f32[768]{0:T(1024)S(1)} %broadcast_divide_fusion.1) | copy-start | bytes 9220
  213.3 57.9 %copy-start.13 = (bf16[2,512,768]{2,1,0:T(8,128)(2,1)S(1)}, bf16[2,512,768]{2,1,0:T(8,128)(2,1)}, u32[]{:S(2)}) copy-start(bf16[2,512,768]{2,1,0:T(8,128)(2,1)} %param.20) | copy-start | bytes 4718596
  213.3 25.9 %collective-permute-start.5 = (bf16[96,3072]{1,0:T(8,128)(2,1)S(1)}, bf16[96,3072]{1,0:T(8,128)(2,1)S(1)}, u32[]{:S(2)}, u32[]{:S(2)}) collective-permute-start(bf16[96,3072]{1,0:T(8,128)(2,1)S(1)} %collective-permute-done.4), channel_id=1, source_target_pairs={{0,1},{1,2},{2,3},{3,4},{4,5},{5,6},{6,7},{7,0},{8,9},{9,10},{10,1... | collective-permute-start | bytes 1769480 | tf_op jit(solution)/shard_map/ppermute | solution.py:23
  239.2 31.1 %collective-permute-start.6 = (bf16[96,3072]{1,0:T(8,128)(2,1)S(1)}, bf16[96,3072]{1,0:T(8,128)(2,1)S(1)}, u32[]{:S(2)}, u32[]{:S(2)}) collective-permute-start(bf16[96,3072]{1,0:T(8,128)(2,1)S(1)} %collective-permute-done.5), channel_id=1, source_target_pairs={{0,1},{1,2},{2,3},{3,4},{4,5},{5,6},{6,7},{7,0},{8,9},{9,10},{10,1... | collective-permute-start | bytes 1769480 | tf_op jit(solution)/shard_map/ppermute | solution.py:23
  315.6 87.3 %copy-start.36 = (f32[2,512]{1,0:T(2,128)}, f32[2,512]{1,0:T(2,128)S(1)}, u32[]{:S(2)}) copy-start(f32[2,512]{1,0:T(2,128)S(1)} %broadcast_multiply_fusion.1) | copy-start | bytes 12292
  316.1 86.8 %copy-start.42 = (f32[2,512]{1,0:T(2,128)}, f32[2,512]{1,0:T(2,128)S(1)}, u32[]{:S(2)}) copy-start(f32[2,512]{1,0:T(2,128)S(1)} %fusion.66) | copy-start | bytes 12292
  409.2 242.0 %reduce-scatter.6.cloned.1.call-start = ((), (), s32[]{:S(2)}) async-start(), calls=%async_computation.10 | async-start | bytes 1327104 | tf_op jit(solution)/shard_map/reduce_scatter | solution.py:318
  413.2 77.4 %copy-start.52 = (f32[2,512]{1,0:T(2,128)S(1)}, f32[2,512]{1,0:T(2,128)}, u32[]{:S(2)}) copy-start(f32[2,512]{1,0:T(2,128)} %copy-done.51) | copy-start | bytes 12292
  500.8 50.4 %copy-start.35 = (f32[768]{0:T(1024)S(1)}, f32[768]{0:T(1024)}, u32[]{:S(2)}) copy-start(f32[768]{0:T(1024)} %copy-done.34) | copy-start | bytes 9220
  500.8 52.7 %copy-start.16 = (bf16[2,128,768]{2,1,0:T(8,128)(2,1)S(1)}, bf16[2,128,768]{2,1,0:T(8,128)(2,1)}, u32[]{:S(2)}) copy-start(bf16[2,128,768]{2,1,0:T(8,128)(2,1)} %copy-done.15) | copy-start | bytes 1179652
  502.9 52.2 %copy-start.14 = (bf16[2,512,768]{2,1,0:T(8,128)(2,1)S(1)}, bf16[2,512,768]{2,1,0:T(8,128)(2,1)}, u32[]{:S(2)}) copy-start(bf16[2,512,768]{2,1,0:T(8,128)(2,1)} %param.20) | copy-start | bytes 4718596
  555.1 147.0 %reduce-scatter.8.cloned.1.call-start = ((), (), s32[]{:S(2)}) async-start(), calls=%async_computation.11 | async-start | bytes 3981312 | tf_op jit(solution)/shard_map/reduce_scatter | solution.py:321
  564.2 236.3 %reduce-scatter.14.cloned.1.call-start = ((), (), s32[]{:S(2)}) async-start(), calls=%async_computation.14 | async-start | bytes 5308416 | tf_op jit(solution)/shard_map/reduce_scatter | solution.py:336
  577.3 321.8 %reduce-scatter.12.cloned.1.call-start = ((), (), s32[]{:S(2)}) async-start(), calls=%async_computation.13 | async-start | bytes 5308416 | tf_op jit(solution)/shard_map/reduce_scatter | solution.py:333
  588.4 310.7 %copy-start.18 = (bf16[2,128,768]{2,1,0:T(8,128)(2,1)S(1)}, bf16[2,128,768]{2,1,0:T(8,128)(2,1)}, u32[]{:S(2)}) copy-start(bf16[2,128,768]{2,1,0:T(8,128)(2,1)} %copy-done.17) | copy-start | bytes 1179652
  588.4 362.5 %all-reduce.18.cloned.1.call-start = ((), (), s32[]{:S(2)}) async-start(), calls=%async_computation.15 | async-start | bytes 3833856 | tf_op jit(solution)/shard_map/psum | solution.py:347
  (54 other events, 625.8 us)
Sparse Core Ops, SparseCore 0:
  10.3 51.0 all-gather.5
  63.6 82.8 all-gather.7
  148.7 44.5 all-gather.9
  195.3 99.0 all-gather.11
  296.4 77.9 all-gather.13
  409.3 71.1 reduce-scatter.9
  555.2 64.8 reduce-scatter.5
  623.7 78.2 reduce-scatter.7
  705.7 94.8 reduce-scatter.13
  804.0 94.9 reduce-scatter.11
  901.8 49.1 all-reduce.17
